TPU v7x, 32 devices: a whole 2x2x4 slice. The times are simulated.
32 devices in a mesh: tx: 4 (over x, core), ty: 4 (over z), src: 2 (over y).
Axes of the slice: x: 2, y: 2, z: 4, core: 2. Of those that a mesh axis runs over, the one named last changes fastest.
Arguments:
- spectrum: bfloat16 [2, 512, 512], P(None, ('tx', 'ty'), 'src'), may hold values from -0.0234375 to 0.0234375
- pupil_mask: int32 [256, 256], replicated, may hold values 0 or 1
- source_shifts: int32 [64, 2], P('src'), may hold values from 0 to 256
- source_weights: int32 [64], P('src'), may hold values from 0 to 8, as said below
Outputs:
- acid_level: float32 [2048, 1024], P(('tx', 'src'), 'ty')
Inputs may be any that keep to these rules, and one draw needn't show every extreme that they name: `source_weights`: the 32 consecutive sources of each group (one index of src) hold at least 4 points with weight above 0; some group has all 32 points on.
All inputs are finite; a program needn't handle non-finite values.
Results may differ from a plain program's by a relative error of at most 0.0017.
Values may be sent and summed in bfloat16 or wider, within the bound.
A program may use at most 64 MiB of HBM per device.

v0:
```python
import jax
import jax.numpy as jnp
from jax import lax
from jax.sharding import PartitionSpec as P

FRAME = 2048
BX = 512
BY = 256
diffusion_rate = 0.2
per_turn = 4


def padded_2(cells, sides, width):
    for axis, dim in sides:
        count = lax.axis_size(axis)
        ends = count - 1
        head = lax.slice_in_dim(cells, 0, width, axis=dim)
        tail = lax.slice_in_dim(cells, cells.shape[dim] - width, cells.shape[dim], axis=dim)
        cells = jnp.concatenate(
            [
                lax.ppermute(tail, axis, [(i, (i + 1) % count) for i in range(ends)]),
                cells,
                lax.ppermute(head, axis, [((i + 1) % count, i) for i in range(ends)]),
            ],
            axis=dim,
        )
    return cells


def phase_table(positions, frequency_count, frame_points):
    frequency = jnp.arange(frequency_count, dtype=jnp.int32) - frequency_count // 2
    phase_turns = positions[:, None] * frequency[None, :] % frame_points
    phase_angle = phase_turns.astype(jnp.float32) * (2.0 * jnp.pi / frame_points)
    return (jnp.cos(phase_angle), jnp.sin(phase_angle))


def rotation_table(cosine, sine):
    upper = jnp.concatenate([cosine, -sine], axis=1)
    lower = jnp.concatenate([sine, cosine], axis=1)
    return jnp.concatenate([upper, lower], axis=0).astype(jnp.bfloat16)


def diffuse(level, padded):
    beside = padded[2:, 1:-1] + padded[:-2, 1:-1] + padded[1:-1, 2:] + padded[1:-1, :-2]
    return level + diffusion_rate * (beside - 4.0 * level)


def arrange(shift_rows, weight_rows, slot_count, offset, stride):
    total_rows = weight_rows.shape[0]
    dead_flag = (weight_rows <= 0).astype(jnp.int32)
    live_order = jnp.argsort(dead_flag * total_rows + jnp.arange(total_rows, dtype=jnp.int32))
    live_count = jnp.sum(1 - dead_flag)
    pick_slots = offset + stride * jnp.arange(slot_count, dtype=jnp.int32)
    chosen = live_order[pick_slots]
    mine_count = jnp.maximum(live_count - offset + stride - 1, 0) // stride
    return (shift_rows[chosen], weight_rows[chosen], mine_count)


def windows(spectrum_all, pupil_bf, shift_batch, passband):

    def take_window(shift_pair):
        return lax.dynamic_slice(
            spectrum_all, (jnp.int32(0), shift_pair[0], shift_pair[1]), (2, passband, passband)
        )

    return jax.vmap(take_window)(shift_batch) * pupil_bf


def inner_block(window_cut, col_table):
    batch_count, _, passband, _ = window_cut.shape
    col_count = col_table.shape[1] // 2
    product = jnp.dot(
        window_cut.reshape(batch_count * 2 * passband, passband),
        col_table,
        preferred_element_type=jnp.float32,
    )
    product = product.reshape(batch_count, 2, passband, 2, col_count)
    real_part = product[:, 0, :, 0] - product[:, 1, :, 1]
    imag_part = product[:, 0, :, 1] + product[:, 1, :, 0]
    stacked = jnp.stack([real_part, imag_part], axis=0).astype(jnp.bfloat16)
    return stacked.transpose(0, 2, 1, 3).reshape(2 * passband, batch_count * col_count)


def power_sum(row_table, block_pair, weight_batch):
    row_total = row_table.shape[0] // 2
    batch_count = weight_batch.shape[0]
    field_pair = jnp.dot(row_table, block_pair, preferred_element_type=jnp.float32)
    square = field_pair[:row_total] ** 2 + field_pair[row_total:] ** 2
    square = square.reshape(row_total, batch_count, -1)
    return jnp.einsum("rbc,b->rc", square, weight_batch.astype(jnp.float32))


def owner_rows(row_count, passband):
    positions = lax.axis_index("tx") * BX + jnp.arange(row_count, dtype=jnp.int32)
    row_cos, row_sin = phase_table(positions, passband, FRAME)
    return rotation_table(row_cos, row_sin)


def body(spectrum, pupil_mask, source_shifts, source_weights):
    partial_spec = lax.all_gather(spectrum, "src", axis=2, tiled=True)
    spectrum_all = lax.all_gather(partial_spec, ("tx", "ty"), axis=1, tiled=True)
    passband = pupil_mask.shape[0]
    pupil_bf = pupil_mask.astype(jnp.bfloat16)
    group_count = lax.axis_size("src")
    slot_count = source_weights.shape[0]
    source_count = slot_count * group_count
    block_rows = BX // group_count
    all_shifts, all_weights = (
        lax.all_gather(source_shifts, "src", axis=0, tiled=True),
        lax.all_gather(source_weights, "src", axis=0, tiled=True),
    )
    chosen_shifts, chosen_weights, mine_count = arrange(
        all_shifts, all_weights, slot_count, lax.axis_index("src"), group_count
    )
    turn_count = (mine_count + per_turn - 1) // per_turn
    columns = lax.axis_index("ty") * BY + jnp.arange(BY, dtype=jnp.int32)
    col_cos, col_sin = phase_table(columns, passband, FRAME)
    col_table = jnp.concatenate([col_cos.T, col_sin.T], axis=1).astype(jnp.bfloat16)
    batch_shifts = chosen_shifts.reshape(slot_count // per_turn, per_turn, 2)
    batch_weights = chosen_weights.reshape(slot_count // per_turn, per_turn)

    def section_one(turn_index):
        return inner_block(
            windows(spectrum_all, pupil_bf, batch_shifts[turn_index], passband), col_table
        )

    row_table = owner_rows(BX, passband)

    def whole_turn(turn_index, running):
        return running + power_sum(row_table, section_one(turn_index), batch_weights[turn_index])

    partial_sum = lax.fori_loop(0, turn_count, whole_turn, jnp.zeros((BX, BY), jnp.float32))
    intensity_sum = lax.psum(partial_sum.astype(jnp.bfloat16), "src").astype(jnp.float32)
    acid_level = 1.0 - jnp.exp(-(intensity_sum / (2.0 * source_count)))
    for repeat in range(2):
        padded = padded_2(acid_level, (("tx", 0), ("ty", 1)), 1)
        acid_level = diffuse(acid_level, padded)
    acid_level = lax.dynamic_slice_in_dim(
        acid_level, lax.axis_index("src") * block_rows, block_rows, 0
    )
    return acid_level


def solution(mesh):
    placed = (P(None, ("tx", "ty"), "src"), P(), P("src", None), P("src"))
    return jax.shard_map(
        body, mesh=mesh, in_specs=placed, out_specs=P(("tx", "src"), "ty"), check_vma=False
    )
```

profile of v0, /device:TPU:0, one launch (start us, length us, event | category | flops | bytes accessed | tf_op | source)
XLA Modules:
  0.0 222.1 jit_solution(6561495545590390177)
XLA Ops:
  6.5 7.2 %all_gather.14 = bf16[2,32,512]{2,1,0:T(8,128)(2,1)} all-gather(bf16[2,32,256]{2,1,0:T(8,128)(2,1)} %param.6), channel_id=1, replica_groups=mesh['tx'=4,'ty'=4,'src'=2] {'src'}, dimensions={2}, use_global_device_ids=true | all-gather | bytes 98304 | tf_op jit(solution)/shard_map/all_gather | solution.py:100
  16.6 4.3 %all-reduce = s32[64]{0:T(128)S(1)} all-reduce(s32[64]{0:T(128)S(1)} %dynamic-update-slice.2), channel_id=1, replica_groups=mesh['tx'=4,'ty'=4,'src'=2] {'src'}, use_global_device_ids=true, to_apply=%add | all-reduce | flops 64 | bytes 512
  25.7 4.5 %all-gather = s32[2,32,2]{1,2,0:T(2,128)S(1)} all-gather(s32[1,32,2]{1,2,0:T(2,128)} %bitcast.113), channel_id=1, replica_groups=mesh['tx'=4,'ty'=4,'src'=2] {'src'}, dimensions={0}, use_global_device_ids=true | all-gather | bytes 768 | tf_op jit(solution)/shard_map/all_gather | solution.py:109
  33.3 2.5 %negate_convert_fusion = (bf16[512,256]{1,0:T(8,128)(2,1)S(1)}, bf16[512,256]{1,0:T(8,128)(2,1)S(1)}, bf16[512,256]{1,0:T(8,128)(2,1)S(1)}) fusion(s32[256]{0:T(256)S(1)} %get-tuple-element.148, s32[512]{0:T(512)S(1)} %iota_add_fusion), kind=kLoop, calls=%fused_computation.69 | loop fusion | flops 2359296 | bytes 789504 | tf_op jit(solution)/shard_map/convert.9
  36.9 15.4 %all-gather.3.cloned.1.call-done = bf16[2,512,512]{2,1,0:T(8,128)(2,1)} async-done(((bf16[2,32,512]{2,1,0:T(8,128)(2,1)}), bf16[2,512,512]{2,1,0:T(8,128)(2,1)}) %all-gather.3.cloned.1.call-update) | async-done | bytes 1048592 | tf_op jit(solution)/shard_map/all_gather | solution.py:101
  52.4 98.3 %while.13 = (s32[]{:T(128)}, f32[512,256]{1,0:T(8,128)S(1)}, s32[]{:T(128)}, s32[8,4,2]{1,2,0:T(2,128)S(1)}, bf16[2,512,512]{2,1,0:T(8,128)(2,1)}, /*index=5*/bf...) while((s32[]{:T(128)}, f32[512,256]{1,0:T(8,128)S(1)}, ...), condition=%wide.region_3.4_spmd, body=%wide.region_2.3_spmd.sunk | while | flops 1617559552 | bytes 34473136 | solution.py:132
  52.6 12.7 %while.14 = (s32[]{:T(128)}, bf16[2,512,512]{2,1,0:T(8,128)(2,1)}, s32[4,3]{1,0:T(4,128)S(1)}, bf16[4,2,256,256]{3,2,1,0:T(8,128)(2,1)S(1)}, s32[]{:T(128)}) while((s32[]{:T(128)}, bf16[2,512,512]{2,1,0:T(8,128)(2,1)}, s32[4,3]{1,0:T(4,128)S(1)}, bf16[4,2,256,256]{3,2,1,0:T(8,128)(2,1)S(1)}, s32[]{:T(128)}) %tuple.54), condition=%wide.while_cond, body=%wide.while_body.sunk | while | flops 2 | bytes 524413 | solution.py:62
  67.4 2.5 %convolution_bitcast_fusion.2 = f32[1024,1024]{0,1:T(8,128)S(1)} fusion(bf16[512,1024]{1,0:T(8,128)(2,1)S(1)} %bitcast.109, bf16[1024,512]{1,0:T(8,128)(2,1)} %get-tuple-element.298), kind=kOutput, calls=%fused_computation.5.clone.1 | convolution fusion | flops 1073741824 | bytes 6291456 | tf_op jit(solution)/shard_map/while/body/dot_general | solution.py:87
  72.2 12.7 %while.14 = (s32[]{:T(128)}, bf16[2,512,512]{2,1,0:T(8,128)(2,1)}, s32[4,3]{1,0:T(4,128)S(1)}, bf16[4,2,256,256]{3,2,1,0:T(8,128)(2,1)S(1)}, s32[]{:T(128)}) while((s32[]{:T(128)}, bf16[2,512,512]{2,1,0:T(8,128)(2,1)}, s32[4,3]{1,0:T(4,128)S(1)}, bf16[4,2,256,256]{3,2,1,0:T(8,128)(2,1)S(1)}, s32[]{:T(128)}) %tuple.54), condition=%wide.while_cond, body=%wide.while_body.sunk | while | flops 2 | bytes 524413 | solution.py:62
  87.1 2.5 %convolution_bitcast_fusion.2 = f32[1024,1024]{0,1:T(8,128)S(1)} fusion(bf16[512,1024]{1,0:T(8,128)(2,1)S(1)} %bitcast.109, bf16[1024,512]{1,0:T(8,128)(2,1)} %get-tuple-element.298), kind=kOutput, calls=%fused_computation.5.clone.1 | convolution fusion | flops 1073741824 | bytes 6291456 | tf_op jit(solution)/shard_map/while/body/dot_general | solution.py:87
  91.9 12.7 %while.14 = (s32[]{:T(128)}, bf16[2,512,512]{2,1,0:T(8,128)(2,1)}, s32[4,3]{1,0:T(4,128)S(1)}, bf16[4,2,256,256]{3,2,1,0:T(8,128)(2,1)S(1)}, s32[]{:T(128)}) while((s32[]{:T(128)}, bf16[2,512,512]{2,1,0:T(8,128)(2,1)}, s32[4,3]{1,0:T(4,128)S(1)}, bf16[4,2,256,256]{3,2,1,0:T(8,128)(2,1)S(1)}, s32[]{:T(128)}) %tuple.54), condition=%wide.while_cond, body=%wide.while_body.sunk | while | flops 2 | bytes 524413 | solution.py:62
  106.7 2.5 %convolution_bitcast_fusion.2 = f32[1024,1024]{0,1:T(8,128)S(1)} fusion(bf16[512,1024]{1,0:T(8,128)(2,1)S(1)} %bitcast.109, bf16[1024,512]{1,0:T(8,128)(2,1)} %get-tuple-element.298), kind=kOutput, calls=%fused_computation.5.clone.1 | convolution fusion | flops 1073741824 | bytes 6291456 | tf_op jit(solution)/shard_map/while/body/dot_general | solution.py:87
  111.5 12.7 %while.14 = (s32[]{:T(128)}, bf16[2,512,512]{2,1,0:T(8,128)(2,1)}, s32[4,3]{1,0:T(4,128)S(1)}, bf16[4,2,256,256]{3,2,1,0:T(8,128)(2,1)S(1)}, s32[]{:T(128)}) while((s32[]{:T(128)}, bf16[2,512,512]{2,1,0:T(8,128)(2,1)}, s32[4,3]{1,0:T(4,128)S(1)}, bf16[4,2,256,256]{3,2,1,0:T(8,128)(2,1)S(1)}, s32[]{:T(128)}) %tuple.54), condition=%wide.while_cond, body=%wide.while_body.sunk | while | flops 2 | bytes 524413 | solution.py:62
  126.4 2.5 %convolution_bitcast_fusion.2 = f32[1024,1024]{0,1:T(8,128)S(1)} fusion(bf16[512,1024]{1,0:T(8,128)(2,1)S(1)} %bitcast.109, bf16[1024,512]{1,0:T(8,128)(2,1)} %get-tuple-element.298), kind=kOutput, calls=%fused_computation.5.clone.1 | convolution fusion | flops 1073741824 | bytes 6291456 | tf_op jit(solution)/shard_map/while/body/dot_general | solution.py:87
  131.2 12.7 %while.14 = (s32[]{:T(128)}, bf16[2,512,512]{2,1,0:T(8,128)(2,1)}, s32[4,3]{1,0:T(4,128)S(1)}, bf16[4,2,256,256]{3,2,1,0:T(8,128)(2,1)S(1)}, s32[]{:T(128)}) while((s32[]{:T(128)}, bf16[2,512,512]{2,1,0:T(8,128)(2,1)}, s32[4,3]{1,0:T(4,128)S(1)}, bf16[4,2,256,256]{3,2,1,0:T(8,128)(2,1)S(1)}, s32[]{:T(128)}) %tuple.54), condition=%wide.while_cond, body=%wide.while_body.sunk | while | flops 2 | bytes 524413 | solution.py:62
  146.0 2.5 %convolution_bitcast_fusion.2 = f32[1024,1024]{0,1:T(8,128)S(1)} fusion(bf16[512,1024]{1,0:T(8,128)(2,1)S(1)} %bitcast.109, bf16[1024,512]{1,0:T(8,128)(2,1)} %get-tuple-element.298), kind=kOutput, calls=%fused_computation.5.clone.1 | convolution fusion | flops 1073741824 | bytes 6291456 | tf_op jit(solution)/shard_map/while/body/dot_general | solution.py:87
  151.4 22.4 %all-reduce.3.cloned.1.call-done = bf16[512,256]{1,0:T(8,128)(2,1)} async-done(((bf16[512,256]{1,0:T(8,128)(2,1)}), bf16[512,256]{1,0:T(8,128)(2,1)}) %all-reduce.3.cloned.1.call-update) | async-done | bytes 262160 | tf_op jit(solution)/shard_map/psum | solution.py:133
  177.5 3.5 %collective-permute-done = f32[1,256]{1,0:T(1,128)S(1)} collective-permute-done((f32[1,256]{1,0:T(1,128)S(1)}, f32[1,256]{1,0:T(1,128)S(1)}, u32[]{:S(2)}, u32[]{:S(2)}) %collective-permute-start) | collective-permute-done | bytes 1056 | tf_op jit(solution)/shard_map/ppermute | solution.py:23
  182.5 4.6 %collective-permute-start.3 = (f32[514,1]{1,0:T(8,128)S(1)}, f32[514,1]{1,0:T(8,128)S(1)}, u32[]{:S(2)}, u32[]{:S(2)}) collective-permute-start(f32[514,1]{1,0:T(8,128)S(1)} %get-tuple-element.136), channel_id=1, source_target_pairs={{0,2},{2,4},{4,6},{1,3},{3,5},{5,7},{8,10},{10,12},{12,14},{9,11},... | collective-permute-start | bytes 6176 | tf_op jit(solution)/shard_map/ppermute | solution.py:21
  187.0 3.9 %collective-permute-done.2 = f32[514,1]{1,0:T(8,128)S(1)} collective-permute-done((f32[514,1]{1,0:T(8,128)S(1)}, f32[514,1]{1,0:T(8,128)S(1)}, u32[]{:S(2)}, u32[]{:S(2)}) %collective-permute-start.2) | collective-permute-done | bytes 2088 | tf_op jit(solution)/shard_map/ppermute | solution.py:23
  193.2 3.1 %collective-permute-start.5 = (f32[1,256]{1,0:T(1,128)S(1)}, f32[1,256]{1,0:T(1,128)S(1)}, u32[]{:S(2)}, u32[]{:S(2)}) collective-permute-start(f32[1,256]{1,0:T(1,128)S(1)} %get-tuple-element.137), channel_id=1, source_target_pairs={{0,8},{8,16},{16,24},{1,9},{9,17},{17,25},{2,10},{10,18},{18,26},{... | collective-permute-start | bytes 3080 | tf_op jit(solution)/shard_map/ppermute | solution.py:21
  199.5 4.1 %collective-permute-start.7 = (f32[514,1]{1,0:T(8,128)S(1)}, f32[514,1]{1,0:T(8,128)S(1)}, u32[]{:S(2)}, u32[]{:S(2)}) collective-permute-start(f32[514,1]{1,0:T(8,128)S(1)} %get-tuple-element.133), channel_id=1, source_target_pairs={{0,2},{2,4},{4,6},{1,3},{3,5},{5,7},{8,10},{10,12},{12,14},{9,11},... | collective-permute-start | bytes 6176 | tf_op jit(solution)/shard_map/ppermute | solution.py:21
  205.2 4.4 %collective-permute-done.7 = f32[514,1]{1,0:T(8,128)S(1)} collective-permute-done((f32[514,1]{1,0:T(8,128)S(1)}, f32[514,1]{1,0:T(8,128)S(1)}, u32[]{:S(2)}, u32[]{:S(2)}) %collective-permute-start.7) | collective-permute-done | bytes 2088 | tf_op jit(solution)/shard_map/ppermute | solution.py:21
  209.5 4.7 %collective-permute-done.6 = f32[514,1]{1,0:T(8,128)S(1)} collective-permute-done((f32[514,1]{1,0:T(8,128)S(1)}, f32[514,1]{1,0:T(8,128)S(1)}, u32[]{:S(2)}, u32[]{:S(2)}) %collective-permute-start.6) | collective-permute-done | bytes 2088 | tf_op jit(solution)/shard_map/ppermute | solution.py:23
  (187 shorter events, 109.0 us)
Async XLA Ops:
  6.5 45.8 %all-gather.3.cloned.1.call-start = ((), (), s32[]{:S(2)}) async-start(), calls=%async_computation | async-start | bytes 1114112 | tf_op jit(solution)/shard_map/all_gather | solution.py:101
  13.8 160.1 %all-reduce.3.cloned.1.call-start = ((), (), s32[]{:S(2)}) async-start(), calls=%async_computation.1 | async-start | bytes 524288 | tf_op jit(solution)/shard_map/psum | solution.py:133
  174.9 2.6 %collective-permute-start.1 = (f32[1,256]{1,0:T(1,128)S(1)}, f32[1,256]{1,0:T(1,128)S(1)}, u32[]{:S(2)}, u32[]{:S(2)}) collective-permute-start(f32[1,256]{1,0:T(1,128)S(1)} %get-tuple-element.139), channel_id=1, source_target_pairs={{0,8},{8,16},{16,24},{1,9},{9,17},{17,25},{2,10},{10,18},{18,26},{... | collective-permute-start | bytes 3080 | tf_op jit(solution)/shard_map/ppermute | solution.py:21
  176.2 4.8 %collective-permute-start = (f32[1,256]{1,0:T(1,128)S(1)}, f32[1,256]{1,0:T(1,128)S(1)}, u32[]{:S(2)}, u32[]{:S(2)}) collective-permute-start(f32[1,256]{1,0:T(1,128)S(1)} %get-tuple-element.140), channel_id=1, source_target_pairs={{8,0},{16,8},{24,16},{9,1},{17,9},{25,17},{10,2},{18,10},{26,18},{... | collective-permute-start | bytes 3080 | tf_op jit(solution)/shard_map/ppermute | solution.py:23
  181.2 9.8 %collective-permute-start.2 = (f32[514,1]{1,0:T(8,128)S(1)}, f32[514,1]{1,0:T(8,128)S(1)}, u32[]{:S(2)}, u32[]{:S(2)}) collective-permute-start(f32[514,1]{1,0:T(8,128)S(1)} %get-tuple-element.135), channel_id=1, source_target_pairs={{2,0},{4,2},{6,4},{3,1},{5,3},{7,5},{10,8},{12,10},{14,12},{11,9},... | collective-permute-start | bytes 6176 | tf_op jit(solution)/shard_map/ppermute | solution.py:23
  182.5 10.2 %collective-permute-start.3 = (f32[514,1]{1,0:T(8,128)S(1)}, f32[514,1]{1,0:T(8,128)S(1)}, u32[]{:S(2)}, u32[]{:S(2)}) collective-permute-start(f32[514,1]{1,0:T(8,128)S(1)} %get-tuple-element.136), channel_id=1, source_target_pairs={{0,2},{2,4},{4,6},{1,3},{3,5},{5,7},{8,10},{10,12},{12,14},{9,11},... | collective-permute-start | bytes 6176 | tf_op jit(solution)/shard_map/ppermute | solution.py:21
  193.2 4.4 %collective-permute-start.5 = (f32[1,256]{1,0:T(1,128)S(1)}, f32[1,256]{1,0:T(1,128)S(1)}, u32[]{:S(2)}, u32[]{:S(2)}) collective-permute-start(f32[1,256]{1,0:T(1,128)S(1)} %get-tuple-element.137), channel_id=1, source_target_pairs={{0,8},{8,16},{16,24},{1,9},{9,17},{17,25},{2,10},{10,18},{18,26},{... | collective-permute-start | bytes 3080 | tf_op jit(solution)/shard_map/ppermute | solution.py:21
  196.3 3.1 %collective-permute-start.4 = (f32[1,256]{1,0:T(1,128)S(1)}, f32[1,256]{1,0:T(1,128)S(1)}, u32[]{:S(2)}, u32[]{:S(2)}) collective-permute-start(f32[1,256]{1,0:T(1,128)S(1)} %get-tuple-element.138), channel_id=1, source_target_pairs={{8,0},{16,8},{24,16},{9,1},{17,9},{25,17},{10,2},{18,10},{26,18},{... | collective-permute-start | bytes 3080 | tf_op jit(solution)/shard_map/ppermute | solution.py:23
  199.5 10.0 %collective-permute-start.7 = (f32[514,1]{1,0:T(8,128)S(1)}, f32[514,1]{1,0:T(8,128)S(1)}, u32[]{:S(2)}, u32[]{:S(2)}) collective-permute-start(f32[514,1]{1,0:T(8,128)S(1)} %get-tuple-element.133), channel_id=1, source_target_pairs={{0,2},{2,4},{4,6},{1,3},{3,5},{5,7},{8,10},{10,12},{12,14},{9,11},... | collective-permute-start | bytes 6176 | tf_op jit(solution)/shard_map/ppermute | solution.py:21
  203.7 10.6 %collective-permute-start.6 = (f32[514,1]{1,0:T(8,128)S(1)}, f32[514,1]{1,0:T(8,128)S(1)}, u32[]{:S(2)}, u32[]{:S(2)}) collective-permute-start(f32[514,1]{1,0:T(8,128)S(1)} %get-tuple-element.134), channel_id=1, source_target_pairs={{2,0},{4,2},{6,4},{3,1},{5,3},{7,5},{10,8},{12,10},{14,12},{11,9},... | collective-permute-start | bytes 6176 | tf_op jit(solution)/shard_map/ppermute | solution.py:23
Sparse Core Ops, SparseCore 0:
  13.9 38.4 all-gather.2
  151.6 22.2 all-reduce.2
where the time goes:
time: 224 us; the launch traced here: 222 us
  local copies, waits for them, and re-layouts  76.7 us (34%)
  waiting for transfers between devices  57.8 us (26%)
  matrix products  19.9 us (9%)
  starting transfers between devices  18.3 us (8%)
  other arithmetic  17.5 us (8%)
  blocking collectives  15.9 us (7%)
  between operations  14.9 us (7%)
    gather x60, local copies, waits for them, and re-layouts  62.8 us
    psum x1, waiting for transfers between devices, body(): lax.psum(partial_sum.astype(jnp.bfloat16), 'src').astype(jnp.float32)  22.4 us
    all_gather x1, waiting for transfers between devices, body(): lax.all_gather(partial_spec, ('tx', 'ty'), axis=1, tiled=True)  15.4 us
    ppermute x4, waiting for transfers between devices, padded_2(): lax.ppermute(head, axis, [((i + 1) % count, i) for i in range(ends)])  13.8 us
    ppermute x4, starting transfers between devices, padded_2(): lax.ppermute(tail, axis, [(i, (i + 1) % count) for i in range(ends)])  13.1 us
    dot_general x5, matrix products, power_sum(): jnp.dot(row_table, block_pair, preferred_element_type=jnp.float32)  12.7 us
    all_gather x1, blocking collectives, body(): partial_spec = lax.all_gather(spectrum, 'src', axis=2, tiled=True)  7.21 us
    ppermute x4, waiting for transfers between devices, padded_2(): lax.ppermute(tail, axis, [(i, (i + 1) % count) for i in range(ends)])  6.11 us
  transfers between devices with their start and end apart: 10, of which 8 were waited for; matrix products, arithmetic and copies ran while one was open for 6% of the time, Pallas kernels for 0%

commit v1 on v0

--- a/solution.py
+++ b/solution.py
@@ -98,7 +98,8 @@
 
 def body(spectrum, pupil_mask, source_shifts, source_weights):
     partial_spec = lax.all_gather(spectrum, "src", axis=2, tiled=True)
-    spectrum_all = lax.all_gather(partial_spec, ("tx", "ty"), axis=1, tiled=True)
+    tiles = lax.all_gather(partial_spec, ("tx", "ty"))
+    spectrum_all = jnp.concatenate(tiles, axis=1)
     passband = pupil_mask.shape[0]
     pupil_bf = pupil_mask.astype(jnp.bfloat16)
     group_count = lax.axis_size("src")

time: 224 us -> 210 us (0.938)
  local copies, waits for them, and re-layouts: 76.7 us -> 62.8 us
    gather x60, local copies, waits for them, and re-layouts: 62.8 us -> 41 us
    while x10 -> x30, local copies, waits for them, and re-layouts: 1.55 us -> 7.29 us
where the time goes in v1:
time: 210 us; the launch traced here: 209 us
  local copies, waits for them, and re-layouts  62.8 us (30%)
  waiting for transfers between devices  57.7 us (27%)
  matrix products  19.9 us (9%)
  other arithmetic  18.6 us (9%)
  starting transfers between devices  18.3 us (9%)
  blocking collectives  15.9 us (8%)
  between operations  14.9 us (7%)
    gather x60, local copies, waits for them, and re-layouts  41 us
    psum x1, waiting for transfers between devices, body(): lax.psum(partial_sum.astype(jnp.bfloat16), 'src').astype(jnp.float32)  22.4 us
    all_gather x1, waiting for transfers between devices, body(): tiles = lax.all_gather(partial_spec, ('tx', 'ty'))  15.3 us
    ppermute x4, waiting for transfers between devices, padded_2(): lax.ppermute(head, axis, [((i + 1) % count, i) for i in range(ends)])  13.8 us
    ppermute x4, starting transfers between devices, padded_2(): lax.ppermute(tail, axis, [(i, (i + 1) % count) for i in range(ends)])  13.1 us
    dot_general x5, matrix products, power_sum(): jnp.dot(row_table, block_pair, preferred_element_type=jnp.float32)  12.7 us
    while x30, local copies, waits for them, and re-layouts  7.29 us
    all_gather x1, blocking collectives, body(): partial_spec = lax.all_gather(spectrum, 'src', axis=2, tiled=True)  7.21 us
  transfers between devices with their start and end apart: 10, of which 8 were waited for; matrix products, arithmetic and copies ran while one was open for 6% of the time, Pallas kernels for 0%

profile of v1, /device:TPU:0, one launch (start us, length us, event | category | flops | bytes accessed | tf_op | source)
XLA Modules:
  0.0 208.9 jit_solution(5202381645745692257)
XLA Ops:
  6.5 7.2 %all_gather.17 = bf16[2,32,512]{2,1,0:T(8,128)(2,1)} all-gather(bf16[2,32,256]{2,1,0:T(8,128)(2,1)} %param.6), channel_id=1, replica_groups=mesh['tx'=4,'ty'=4,'src'=2] {'src'}, dimensions={2}, use_global_device_ids=true | all-gather | bytes 98304 | tf_op jit(solution)/shard_map/all_gather | solution.py:100
  16.6 4.3 %all-reduce = s32[64]{0:T(128)S(1)} all-reduce(s32[64]{0:T(128)S(1)} %dynamic-update-slice.2), channel_id=1, replica_groups=mesh['tx'=4,'ty'=4,'src'=2] {'src'}, use_global_device_ids=true, to_apply=%add | all-reduce | flops 64 | bytes 512
  25.9 4.5 %all-gather.1 = s32[2,32,2]{1,2,0:T(2,128)S(1)} all-gather(s32[1,32,2]{1,2,0:T(2,128)} %bitcast.119), channel_id=1, replica_groups=mesh['tx'=4,'ty'=4,'src'=2] {'src'}, dimensions={0}, use_global_device_ids=true | all-gather | bytes 768 | tf_op jit(solution)/shard_map/all_gather | solution.py:110
  33.4 2.5 %negate_convert_fusion = (bf16[512,256]{1,0:T(8,128)(2,1)S(1)}, bf16[512,256]{1,0:T(8,128)(2,1)S(1)}, bf16[512,256]{1,0:T(8,128)(2,1)S(1)}) fusion(s32[256]{0:T(256)S(1)} %get-tuple-element.148, s32[512]{0:T(512)S(1)} %iota_add_fusion), kind=kLoop, calls=%fused_computation.69 | loop fusion | flops 2359296 | bytes 789504 | tf_op jit(solution)/shard_map/convert.9
  37.0 15.3 %all-gather.4.cloned.1.call-done = bf16[32,32,512]{2,1,0:T(8,128)(2,1)} async-done(((bf16[2,32,512]{2,1,0:T(8,128)(2,1)}), bf16[32,32,512]{2,1,0:T(8,128)(2,1)}) %all-gather.4.cloned.1.call-update) | async-done | bytes 1048592 | tf_op jit(solution)/shard_map/all_gather | solution.py:101
  54.4 82.0 %while.13 = (s32[]{:T(128)}, f32[512,256]{1,0:T(8,128)}, s32[]{:T(128)}, s32[8,4,2]{1,2,0:T(2,128)S(1)}, bf16[2,512,512]{2,1,0:T(8,128)(2,1)S(1)}, /*index=5*/bf...) while((s32[]{:T(128)}, f32[512,256]{1,0:T(8,128)}, ...), condition=%wide.region_3.4_spmd, body=%wide.region_2.3_spmd.sunk | while | flops 1617559552 | bytes 38667496 | solution.py:133
  54.6 8.3 %while.14 = (s32[]{:T(128)}, bf16[2,512,512]{2,1,0:T(8,128)(2,1)S(1)}, s32[4,3]{1,0:T(4,128)S(1)}, bf16[4,2,256,256]{3,2,1,0:T(8,128)(2,1)S(1)}, s32[]{:T(128)}) while((s32[]{:T(128)}, bf16[2,512,512]{2,1,0:T(8,128)(2,1)S(1)}, s32[4,3]{1,0:T(4,128)S(1)}, bf16[4,2,256,256]{3,2,1,0:T(8,128)(2,1)S(1)}, s32[]{:T(128)}) %tuple.54), condition=%wide.while_cond, body=%wide.while_body.sunk | while | flops 2 | bytes 524413 | solution.py:62
  65.0 2.5 %convolution_bitcast_fusion.2 = f32[1024,1024]{0,1:T(8,128)S(1)} fusion(bf16[512,1024]{1,0:T(8,128)(2,1)S(1)} %bitcast.114, bf16[1024,512]{1,0:T(8,128)(2,1)} %get-tuple-element.298), kind=kOutput, calls=%fused_computation.5.clone.1 | convolution fusion | flops 1073741824 | bytes 6291456 | tf_op jit(solution)/shard_map/while/body/dot_general | solution.py:87
  71.0 8.3 %while.14 = (s32[]{:T(128)}, bf16[2,512,512]{2,1,0:T(8,128)(2,1)S(1)}, s32[4,3]{1,0:T(4,128)S(1)}, bf16[4,2,256,256]{3,2,1,0:T(8,128)(2,1)S(1)}, s32[]{:T(128)}) while((s32[]{:T(128)}, bf16[2,512,512]{2,1,0:T(8,128)(2,1)S(1)}, s32[4,3]{1,0:T(4,128)S(1)}, bf16[4,2,256,256]{3,2,1,0:T(8,128)(2,1)S(1)}, s32[]{:T(128)}) %tuple.54), condition=%wide.while_cond, body=%wide.while_body.sunk | while | flops 2 | bytes 524413 | solution.py:62
  81.4 2.5 %convolution_bitcast_fusion.2 = f32[1024,1024]{0,1:T(8,128)S(1)} fusion(bf16[512,1024]{1,0:T(8,128)(2,1)S(1)} %bitcast.114, bf16[1024,512]{1,0:T(8,128)(2,1)} %get-tuple-element.298), kind=kOutput, calls=%fused_computation.5.clone.1 | convolution fusion | flops 1073741824 | bytes 6291456 | tf_op jit(solution)/shard_map/while/body/dot_general | solution.py:87
  87.4 8.3 %while.14 = (s32[]{:T(128)}, bf16[2,512,512]{2,1,0:T(8,128)(2,1)S(1)}, s32[4,3]{1,0:T(4,128)S(1)}, bf16[4,2,256,256]{3,2,1,0:T(8,128)(2,1)S(1)}, s32[]{:T(128)}) while((s32[]{:T(128)}, bf16[2,512,512]{2,1,0:T(8,128)(2,1)S(1)}, s32[4,3]{1,0:T(4,128)S(1)}, bf16[4,2,256,256]{3,2,1,0:T(8,128)(2,1)S(1)}, s32[]{:T(128)}) %tuple.54), condition=%wide.while_cond, body=%wide.while_body.sunk | while | flops 2 | bytes 524413 | solution.py:62
  97.8 2.5 %convolution_bitcast_fusion.2 = f32[1024,1024]{0,1:T(8,128)S(1)} fusion(bf16[512,1024]{1,0:T(8,128)(2,1)S(1)} %bitcast.114, bf16[1024,512]{1,0:T(8,128)(2,1)} %get-tuple-element.298), kind=kOutput, calls=%fused_computation.5.clone.1 | convolution fusion | flops 1073741824 | bytes 6291456 | tf_op jit(solution)/shard_map/while/body/dot_general | solution.py:87
  103.8 8.3 %while.14 = (s32[]{:T(128)}, bf16[2,512,512]{2,1,0:T(8,128)(2,1)S(1)}, s32[4,3]{1,0:T(4,128)S(1)}, bf16[4,2,256,256]{3,2,1,0:T(8,128)(2,1)S(1)}, s32[]{:T(128)}) while((s32[]{:T(128)}, bf16[2,512,512]{2,1,0:T(8,128)(2,1)S(1)}, s32[4,3]{1,0:T(4,128)S(1)}, bf16[4,2,256,256]{3,2,1,0:T(8,128)(2,1)S(1)}, s32[]{:T(128)}) %tuple.54), condition=%wide.while_cond, body=%wide.while_body.sunk | while | flops 2 | bytes 524413 | solution.py:62
  114.2 2.5 %convolution_bitcast_fusion.2 = f32[1024,1024]{0,1:T(8,128)S(1)} fusion(bf16[512,1024]{1,0:T(8,128)(2,1)S(1)} %bitcast.114, bf16[1024,512]{1,0:T(8,128)(2,1)} %get-tuple-element.298), kind=kOutput, calls=%fused_computation.5.clone.1 | convolution fusion | flops 1073741824 | bytes 6291456 | tf_op jit(solution)/shard_map/while/body/dot_general | solution.py:87
  120.2 8.3 %while.14 = (s32[]{:T(128)}, bf16[2,512,512]{2,1,0:T(8,128)(2,1)S(1)}, s32[4,3]{1,0:T(4,128)S(1)}, bf16[4,2,256,256]{3,2,1,0:T(8,128)(2,1)S(1)}, s32[]{:T(128)}) while((s32[]{:T(128)}, bf16[2,512,512]{2,1,0:T(8,128)(2,1)S(1)}, s32[4,3]{1,0:T(4,128)S(1)}, bf16[4,2,256,256]{3,2,1,0:T(8,128)(2,1)S(1)}, s32[]{:T(128)}) %tuple.54), condition=%wide.while_cond, body=%wide.while_body.sunk | while | flops 2 | bytes 524413 | solution.py:62
  130.6 2.5 %convolution_bitcast_fusion.2 = f32[1024,1024]{0,1:T(8,128)S(1)} fusion(bf16[512,1024]{1,0:T(8,128)(2,1)S(1)} %bitcast.114, bf16[1024,512]{1,0:T(8,128)(2,1)} %get-tuple-element.298), kind=kOutput, calls=%fused_computation.5.clone.1 | convolution fusion | flops 1073741824 | bytes 6291456 | tf_op jit(solution)/shard_map/while/body/dot_general | solution.py:87
  138.2 22.4 %all-reduce.3.cloned.1.call-done = bf16[512,256]{1,0:T(8,128)(2,1)} async-done(((bf16[512,256]{1,0:T(8,128)(2,1)}), bf16[512,256]{1,0:T(8,128)(2,1)}) %all-reduce.3.cloned.1.call-update) | async-done | bytes 262160 | tf_op jit(solution)/shard_map/psum | solution.py:134
  164.3 3.4 %collective-permute-done = f32[1,256]{1,0:T(1,128)S(1)} collective-permute-done((f32[1,256]{1,0:T(1,128)S(1)}, f32[1,256]{1,0:T(1,128)S(1)}, u32[]{:S(2)}, u32[]{:S(2)}) %collective-permute-start) | collective-permute-done | bytes 1056 | tf_op jit(solution)/shard_map/ppermute | solution.py:23
  169.3 4.6 %collective-permute-start.3 = (f32[514,1]{1,0:T(8,128)S(1)}, f32[514,1]{1,0:T(8,128)S(1)}, u32[]{:S(2)}, u32[]{:S(2)}) collective-permute-start(f32[514,1]{1,0:T(8,128)S(1)} %get-tuple-element.136), channel_id=1, source_target_pairs={{0,2},{2,4},{4,6},{1,3},{3,5},{5,7},{8,10},{10,12},{12,14},{9,11},... | collective-permute-start | bytes 6176 | tf_op jit(solution)/shard_map/ppermute | solution.py:21
  173.8 3.9 %collective-permute-done.2 = f32[514,1]{1,0:T(8,128)S(1)} collective-permute-done((f32[514,1]{1,0:T(8,128)S(1)}, f32[514,1]{1,0:T(8,128)S(1)}, u32[]{:S(2)}, u32[]{:S(2)}) %collective-permute-start.2) | collective-permute-done | bytes 2088 | tf_op jit(solution)/shard_map/ppermute | solution.py:23
  180.0 3.1 %collective-permute-start.5 = (f32[1,256]{1,0:T(1,128)S(1)}, f32[1,256]{1,0:T(1,128)S(1)}, u32[]{:S(2)}, u32[]{:S(2)}) collective-permute-start(f32[1,256]{1,0:T(1,128)S(1)} %get-tuple-element.137), channel_id=1, source_target_pairs={{0,8},{8,16},{16,24},{1,9},{9,17},{17,25},{2,10},{10,18},{18,26},{... | collective-permute-start | bytes 3080 | tf_op jit(solution)/shard_map/ppermute | solution.py:21
  186.3 4.1 %collective-permute-start.7 = (f32[514,1]{1,0:T(8,128)S(1)}, f32[514,1]{1,0:T(8,128)S(1)}, u32[]{:S(2)}, u32[]{:S(2)}) collective-permute-start(f32[514,1]{1,0:T(8,128)S(1)} %get-tuple-element.133), channel_id=1, source_target_pairs={{0,2},{2,4},{4,6},{1,3},{3,5},{5,7},{8,10},{10,12},{12,14},{9,11},... | collective-permute-start | bytes 6176 | tf_op jit(solution)/shard_map/ppermute | solution.py:21
  191.9 4.4 %collective-permute-done.7 = f32[514,1]{1,0:T(8,128)S(1)} collective-permute-done((f32[514,1]{1,0:T(8,128)S(1)}, f32[514,1]{1,0:T(8,128)S(1)}, u32[]{:S(2)}, u32[]{:S(2)}) %collective-permute-start.7) | collective-permute-done | bytes 2088 | tf_op jit(solution)/shard_map/ppermute | solution.py:21
  196.3 4.7 %collective-permute-done.6 = f32[514,1]{1,0:T(8,128)S(1)} collective-permute-done((f32[514,1]{1,0:T(8,128)S(1)}, f32[514,1]{1,0:T(8,128)S(1)}, u32[]{:S(2)}, u32[]{:S(2)}) %collective-permute-start.6) | collective-permute-done | bytes 2088 | tf_op jit(solution)/shard_map/ppermute | solution.py:23
  (208 shorter events, 96.0 us)
Async XLA Ops:
  6.5 45.8 %all-gather.4.cloned.1.call-start = ((), (), s32[]{:S(2)}) async-start(), calls=%async_computation.1 | async-start | bytes 1114112 | tf_op jit(solution)/shard_map/all_gather | solution.py:101
  13.8 146.9 %all-reduce.3.cloned.1.call-start = ((), (), s32[]{:S(2)}) async-start(), calls=%async_computation | async-start | bytes 524288 | tf_op jit(solution)/shard_map/psum | solution.py:134
  68.9 1.0 copy-start
  70.0 0.8 copy-start.1
  85.3 1.0 copy-start
  86.4 0.8 copy-start.1
  101.7 1.0 copy-start
  102.8 0.8 copy-start.1
  118.1 1.0 copy-start
  119.2 0.8 copy-start.1
  134.5 1.0 copy-start
  135.6 0.8 copy-start.1
  161.7 2.6 %collective-permute-start.1 = (f32[1,256]{1,0:T(1,128)S(1)}, f32[1,256]{1,0:T(1,128)S(1)}, u32[]{:S(2)}, u32[]{:S(2)}) collective-permute-start(f32[1,256]{1,0:T(1,128)S(1)} %get-tuple-element.139), channel_id=1, source_target_pairs={{0,8},{8,16},{16,24},{1,9},{9,17},{17,25},{2,10},{10,18},{18,26},{... | collective-permute-start | bytes 3080 | tf_op jit(solution)/shard_map/ppermute | solution.py:21
  163.0 4.8 %collective-permute-start = (f32[1,256]{1,0:T(1,128)S(1)}, f32[1,256]{1,0:T(1,128)S(1)}, u32[]{:S(2)}, u32[]{:S(2)}) collective-permute-start(f32[1,256]{1,0:T(1,128)S(1)} %get-tuple-element.140), channel_id=1, source_target_pairs={{8,0},{16,8},{24,16},{9,1},{17,9},{25,17},{10,2},{18,10},{26,18},{... | collective-permute-start | bytes 3080 | tf_op jit(solution)/shard_map/ppermute | solution.py:23
  168.0 9.8 %collective-permute-start.2 = (f32[514,1]{1,0:T(8,128)S(1)}, f32[514,1]{1,0:T(8,128)S(1)}, u32[]{:S(2)}, u32[]{:S(2)}) collective-permute-start(f32[514,1]{1,0:T(8,128)S(1)} %get-tuple-element.135), channel_id=1, source_target_pairs={{2,0},{4,2},{6,4},{3,1},{5,3},{7,5},{10,8},{12,10},{14,12},{11,9},... | collective-permute-start | bytes 6176 | tf_op jit(solution)/shard_map/ppermute | solution.py:23
  169.3 10.2 %collective-permute-start.3 = (f32[514,1]{1,0:T(8,128)S(1)}, f32[514,1]{1,0:T(8,128)S(1)}, u32[]{:S(2)}, u32[]{:S(2)}) collective-permute-start(f32[514,1]{1,0:T(8,128)S(1)} %get-tuple-element.136), channel_id=1, source_target_pairs={{0,2},{2,4},{4,6},{1,3},{3,5},{5,7},{8,10},{10,12},{12,14},{9,11},... | collective-permute-start | bytes 6176 | tf_op jit(solution)/shard_map/ppermute | solution.py:21
  180.0 4.4 %collective-permute-start.5 = (f32[1,256]{1,0:T(1,128)S(1)}, f32[1,256]{1,0:T(1,128)S(1)}, u32[]{:S(2)}, u32[]{:S(2)}) collective-permute-start(f32[1,256]{1,0:T(1,128)S(1)} %get-tuple-element.137), channel_id=1, source_target_pairs={{0,8},{8,16},{16,24},{1,9},{9,17},{17,25},{2,10},{10,18},{18,26},{... | collective-permute-start | bytes 3080 | tf_op jit(solution)/shard_map/ppermute | solution.py:21
  183.1 3.1 %collective-permute-start.4 = (f32[1,256]{1,0:T(1,128)S(1)}, f32[1,256]{1,0:T(1,128)S(1)}, u32[]{:S(2)}, u32[]{:S(2)}) collective-permute-start(f32[1,256]{1,0:T(1,128)S(1)} %get-tuple-element.138), channel_id=1, source_target_pairs={{8,0},{16,8},{24,16},{9,1},{17,9},{25,17},{10,2},{18,10},{26,18},{... | collective-permute-start | bytes 3080 | tf_op jit(solution)/shard_map/ppermute | solution.py:23
  186.3 10.0 %collective-permute-start.7 = (f32[514,1]{1,0:T(8,128)S(1)}, f32[514,1]{1,0:T(8,128)S(1)}, u32[]{:S(2)}, u32[]{:S(2)}) collective-permute-start(f32[514,1]{1,0:T(8,128)S(1)} %get-tuple-element.133), channel_id=1, source_target_pairs={{0,2},{2,4},{4,6},{1,3},{3,5},{5,7},{8,10},{10,12},{12,14},{9,11},... | collective-permute-start | bytes 6176 | tf_op jit(solution)/shard_map/ppermute | solution.py:21
  190.4 10.6 %collective-permute-start.6 = (f32[514,1]{1,0:T(8,128)S(1)}, f32[514,1]{1,0:T(8,128)S(1)}, u32[]{:S(2)}, u32[]{:S(2)}) collective-permute-start(f32[514,1]{1,0:T(8,128)S(1)} %get-tuple-element.134), channel_id=1, source_target_pairs={{2,0},{4,2},{6,4},{3,1},{5,3},{7,5},{10,8},{12,10},{14,12},{11,9},... | collective-permute-start | bytes 6176 | tf_op jit(solution)/shard_map/ppermute | solution.py:23
Sparse Core Ops, SparseCore 0:
  13.9 38.3 all-gather.3
  138.4 22.2 all-reduce.2
